TPU v7x, 256 devices: a whole 4x4x8 slice. The times are simulated.
256 devices in a mesh: freq: 8 (over y, core), tcol: 32 (over z, x).
Axes of the slice: x: 4, y: 4, z: 8, core: 2. Of those that a mesh axis runs over, the one named last changes fastest.
Arguments:
- data: bfloat16 [8, 2, 16384, 128], P('freq', None, 'tcol'), may hold values from -6 to 6
- left_factor: bfloat16 [8, 2, 16384, 1024], P('freq', None, 'tcol'), may hold values from -0.125 to 0.125
- right_factor: bfloat16 [8, 2, 16384, 1024], P('freq', None, 'tcol'), may hold values from -0.1875 to 0.1875
- ranks: int32 [8, 32, 32], P('freq'), may hold values from 1 to 32
- freq_index: int32 [8], P('freq'), may hold values from 0 to 229
Outputs:
- wavefield: float32 [8, 2, 16384, 128], P('freq', None, 'tcol')
- residual: float32 [8, 2, 16384, 128], P('freq', None, 'tcol')
Inputs may be any that keep to these rules, and one draw needn't show every extreme that they name: `ranks`: the rank of each tile; factor columns at or beyond it are not part of the kernel.
All inputs are finite; a program needn't handle non-finite values.
Results may differ from a plain program's by a relative error of at most 0.006.
Values may be sent and summed in bfloat16 or wider, within the bound.
A program may use at most 64 MiB of HBM per device.

v0:
```python
import jax
import jax.numpy as jnp
from jax import lax
from jax.sharding import Mesh
from jax.sharding import PartitionSpec as P

ITERS = 3
TCOL = ("tcol_0", "tcol_1")
FREQ_TCOL = ("freq_0", "freq_1", "tcol_0", "tcol_1")
FREQ = ("freq_0", "freq_1")


def over_axes(shard, axes):
    for axis in axes:
        shard = lax.psum(shard, axis)
    return shard


def conj_left(factor, field):
    first = jnp.einsum(
        "ftq,fts->fqs", factor[:, 0], field[:, 0], preferred_element_type=jnp.float32
    )
    second = jnp.einsum(
        "ftq,fts->fqs", factor[:, 1], field[:, 1], preferred_element_type=jnp.float32
    )
    third = jnp.einsum(
        "ftq,fts->fqs", factor[:, 0], field[:, 1], preferred_element_type=jnp.float32
    )
    fourth = jnp.einsum(
        "ftq,fts->fqs", factor[:, 1], field[:, 0], preferred_element_type=jnp.float32
    )
    return jnp.stack([first + second, third - fourth], 1)


def plain_right(factor, coeffs):
    first = jnp.einsum(
        "ftq,fqs->fts", factor[:, 0], coeffs[:, 0], preferred_element_type=jnp.float32
    )
    second = jnp.einsum(
        "ftq,fqs->fts", factor[:, 1], coeffs[:, 1], preferred_element_type=jnp.float32
    )
    third = jnp.einsum(
        "ftq,fqs->fts", factor[:, 0], coeffs[:, 1], preferred_element_type=jnp.float32
    )
    fourth = jnp.einsum(
        "ftq,fqs->fts", factor[:, 1], coeffs[:, 0], preferred_element_type=jnp.float32
    )
    return jnp.stack([first - second, third + fourth], 1)


def body(data, left_factor, right_factor, ranks, freq_index):
    ntile = lax.axis_size(TCOL)
    here = lax.axis_index(TCOL)
    rank_width = left_factor.shape[3] // ntile
    levels = jnp.arange(rank_width)[None, None, :]
    column_ranks = lax.dynamic_slice_in_dim(ranks, here, 1, 2)[:, :, 0]
    row_ranks = lax.dynamic_slice_in_dim(ranks, here, 1, 1)[:, 0, :]
    colmask = (levels < column_ranks[:, :, None]).astype(jnp.float32).reshape(ranks.shape[0], -1)
    rowmask = (levels < row_ranks[:, :, None]).astype(jnp.float32).reshape(ranks.shape[0], -1)
    damping = (0.1 + 0.9 * freq_index.astype(jnp.float32) / 229.0)[:, None, None, None]
    residual = data.astype(jnp.float32)
    wavefield = jnp.zeros_like(residual)
    direction = jnp.zeros_like(residual)
    image = jnp.zeros_like(residual)
    for step in range(ITERS):
        coeffs = conj_left(left_factor, residual.astype(jnp.bfloat16))
        coeffs = (coeffs * rowmask[:, None, :, None]).astype(jnp.bfloat16)
        arrived = lax.all_to_all(coeffs, TCOL, split_axis=2, concat_axis=2, tiled=True)
        gradient = plain_right(right_factor, arrived) - damping * wavefield
        forward_coeffs = conj_left(right_factor, gradient.astype(jnp.bfloat16))
        forward_coeffs = (forward_coeffs * colmask[:, None, :, None]).astype(jnp.bfloat16)
        forward_arrived = lax.all_to_all(
            forward_coeffs, TCOL, split_axis=2, concat_axis=2, tiled=True
        )
        moved = plain_right(left_factor, forward_arrived)
        partial_sums = jnp.stack(
            [
                jnp.sum(moved * moved + damping * gradient * gradient, axis=(0, 1, 2)),
                jnp.sum(moved * image + damping * gradient * direction, axis=(0, 1, 2)),
                jnp.sum(image * image + damping * direction * direction, axis=(0, 1, 2)),
                jnp.sum(moved * residual - damping * gradient * wavefield, axis=(0, 1, 2)),
                jnp.sum(image * residual - damping * direction * wavefield, axis=(0, 1, 2)),
            ]
        )
        totals = over_axes(partial_sums, FREQ_TCOL)
        a11, a12, a22, b1, b2 = (totals[0], totals[1], totals[2], totals[3], totals[4])
        if step == 0:
            alpha = b1 / (1.1 * a11)
            beta = jnp.zeros_like(alpha)
        else:
            first = 1.1 * a11
            second = 1.1 * a22
            determinant = first * second - a12 * a12
            alpha = (b1 * second - a12 * b2) / determinant
            beta = (first * b2 - a12 * b1) / determinant
        direction = alpha * gradient + beta * direction
        image = alpha * moved + beta * image
        wavefield = wavefield + direction
        residual = residual - image
    return (wavefield, residual)


def solution(mesh):
    split = Mesh(mesh.devices.reshape(4, 2, 8, 4), ("freq_0", "freq_1", "tcol_0", "tcol_1"))
    return jax.shard_map(
        body,
        mesh=split,
        in_specs=(
            P(FREQ, None, TCOL, None),
            P(FREQ, None, TCOL, None),
            P(FREQ, None, TCOL, None),
            P(FREQ, None, None),
            P(FREQ),
        ),
        out_specs=(P(FREQ, None, TCOL, None), P(FREQ, None, TCOL, None)),
        check_vma=False,
    )
```

profile of v0, /device:TPU:1, one launch (start us, length us, event | category | flops | bytes accessed | tf_op | source)
XLA Modules:
  0.0 284.0 jit_solution(11496676077724546379)
XLA Ops:
  1.5 2.5 fusion.98
  4.0 1.7 fusion.100
  6.1 1.5 fusion.1
  8.3 1.3 copy.46
  9.7 11.9 %all-to-all-start = ((bf16[1,2,1024,128]{3,1,0,2:T(2,128)(2,1)}), bf16[1,2,1024,128]{3,1,0,2:T(2,128)(2,1)S(1)}, u32[]{:S(2)}, u32[]{:S(2)}) async-start(bf16[1,2,1024,128]{3,1,0,2:T(2,128)(2,1)} %copy.46), calls=%async_computation | async-start | bytes 1048576 | tf_op jit(solution)/shard_map/all_to_all | solution.py:68
  22.2 15.6 %all-to-all-done = bf16[1,2,1024,128]{3,1,0,2:T(2,128)(2,1)S(1)} async-done(((bf16[1,2,1024,128]{3,1,0,2:T(2,128)(2,1)}), bf16[1,2,1024,128]{3,1,0,2:T(2,128)(2,1)S(1)}, u32[]{:S(2)}, u32[]{:S(2)}) %all-to-all-start) | async-done | bytes 524320 | tf_op jit(solution)/shard_map/all_to_all | solution.py:68
  42.0 1.1 copy.49
  43.1 5.3 %all-to-all-start.1 = ((bf16[1,2,1024,128]{3,1,0,2:T(2,128)(2,1)}), bf16[1,2,1024,128]{3,1,0,2:T(2,128)(2,1)S(1)}, u32[]{:S(2)}, u32[]{:S(2)}) async-start(bf16[1,2,1024,128]{3,1,0,2:T(2,128)(2,1)} %copy.49), calls=%async_computation.1 | async-start | bytes 1048576 | tf_op jit(solution)/shard_map/all_to_all | solution.py:72
  49.5 14.1 %all-to-all-done.1 = bf16[1,2,1024,128]{3,1,0,2:T(2,128)(2,1)S(1)} async-done(((bf16[1,2,1024,128]{3,1,0,2:T(2,128)(2,1)}), bf16[1,2,1024,128]{3,1,0,2:T(2,128)(2,1)S(1)}, u32[]{:S(2)}, u32[]{:S(2)}) %all-to-all-start.1) | async-done | bytes 524320 | tf_op jit(solution)/shard_map/all_to_all | solution.py:72
  67.6 8.7 %psum.84 = f32[5,128]{1,0:T(8,128)S(1)} all-reduce(f32[5,128]{1,0:T(8,128)S(1)} %stack.179), channel_id=1, replica_groups=mesh['freq_0'=4,'freq_1'=2,'tcol_0'=8,'tcol_1'=4] {'freq_0'}, use_global_device_ids=true, to_apply=%region_4.0 | all-reduce | flops 640 | bytes 5120 | tf_op jit(solution)/shard_map/psum | solution.py:15
  76.3 7.7 %psum.85 = f32[5,128]{1,0:T(8,128)S(1)} all-reduce(f32[5,128]{1,0:T(8,128)S(1)} %psum.84), channel_id=1, replica_groups=mesh['freq_0'=4,'freq_1'=2,'tcol_0'=8,'tcol_1'=4] {'freq_1'}, use_global_device_ids=true, to_apply=%region_5.0 | all-reduce | flops 640 | bytes 5120 | tf_op jit(solution)/shard_map/psum | solution.py:15
  84.1 11.6 %psum.86 = f32[5,128]{1,0:T(8,128)S(1)} all-reduce(f32[5,128]{1,0:T(8,128)S(1)} %psum.85), channel_id=1, replica_groups=mesh['freq_0'=4,'freq_1'=2,'tcol_0'=8,'tcol_1'=4] {'tcol_0'}, use_global_device_ids=true, to_apply=%region_6.0 | all-reduce | flops 640 | bytes 5120 | tf_op jit(solution)/shard_map/psum | solution.py:15
  95.7 7.0 %psum.87 = f32[5,128]{1,0:T(8,128)S(1)} all-reduce(f32[5,128]{1,0:T(8,128)S(1)} %psum.86), channel_id=1, replica_groups=mesh['freq_0'=4,'freq_1'=2,'tcol_0'=8,'tcol_1'=4] {'tcol_1'}, use_global_device_ids=true, to_apply=%region_7.0 | all-reduce | flops 640 | bytes 5120 | tf_op jit(solution)/shard_map/psum | solution.py:15
  102.9 1.9 fusion.90
  107.2 17.6 %all_to_all.30 = bf16[1,2,1024,128]{3,1,0,2:T(2,128)(2,1)S(1)} all-to-all(bf16[1,2,1024,128]{3,1,0,2:T(2,128)(2,1)S(1)} %copy.57), channel_id=1, replica_groups=mesh['freq_0'=4,'freq_1'=2,'tcol_0'=8,'tcol_1'=4] {'tcol_0','tcol_1'}, dimensions={2} | all-to-all | bytes 1048576 | tf_op jit(solution)/shard_map/all_to_all | solution.py:68
  129.9 2.0 copy.60
  131.9 16.7 %all_to_all.31 = bf16[1,2,1024,128]{3,1,0,2:T(2,128)(2,1)S(1)} all-to-all(bf16[1,2,1024,128]{3,1,0,2:T(2,128)(2,1)} %copy.60), channel_id=1, replica_groups=mesh['freq_0'=4,'freq_1'=2,'tcol_0'=8,'tcol_1'=4] {'tcol_0','tcol_1'}, dimensions={2} | all-to-all | bytes 1048576 | tf_op jit(solution)/shard_map/all_to_all | solution.py:72
  152.5 6.0 %psum.88 = f32[5,128]{1,0:T(8,128)S(1)} all-reduce(f32[5,128]{1,0:T(8,128)S(1)} %stack.197), channel_id=1, replica_groups=mesh['freq_0'=4,'freq_1'=2,'tcol_0'=8,'tcol_1'=4] {'freq_0'}, use_global_device_ids=true, to_apply=%region_13.0 | all-reduce | flops 640 | bytes 5120 | tf_op jit(solution)/shard_map/psum | solution.py:15
  158.5 12.7 %psum.89 = f32[5,128]{1,0:T(8,128)S(1)} all-reduce(f32[5,128]{1,0:T(8,128)S(1)} %psum.88), channel_id=1, replica_groups=mesh['freq_0'=4,'freq_1'=2,'tcol_0'=8,'tcol_1'=4] {'freq_1'}, use_global_device_ids=true, to_apply=%region_14.0 | all-reduce | flops 640 | bytes 5120 | tf_op jit(solution)/shard_map/psum | solution.py:15
  171.2 11.6 %psum.90 = f32[5,128]{1,0:T(8,128)S(1)} all-reduce(f32[5,128]{1,0:T(8,128)S(1)} %psum.89), channel_id=1, replica_groups=mesh['freq_0'=4,'freq_1'=2,'tcol_0'=8,'tcol_1'=4] {'tcol_0'}, use_global_device_ids=true, to_apply=%region_15.0 | all-reduce | flops 640 | bytes 5120 | tf_op jit(solution)/shard_map/psum | solution.py:15
  182.8 6.9 %psum.91 = f32[5,128]{1,0:T(8,128)S(1)} all-reduce(f32[5,128]{1,0:T(8,128)S(1)} %psum.90), channel_id=1, replica_groups=mesh['freq_0'=4,'freq_1'=2,'tcol_0'=8,'tcol_1'=4] {'tcol_1'}, use_global_device_ids=true, to_apply=%region_16.0 | all-reduce | flops 640 | bytes 5120 | tf_op jit(solution)/shard_map/psum | solution.py:15
  189.7 2.4 fusion.186
  195.1 17.6 %all_to_all.32 = bf16[1,2,1024,128]{3,1,0,2:T(2,128)(2,1)S(1)} all-to-all(bf16[1,2,1024,128]{3,1,0,2:T(2,128)(2,1)S(1)} %copy.67), channel_id=1, replica_groups=mesh['freq_0'=4,'freq_1'=2,'tcol_0'=8,'tcol_1'=4] {'tcol_0','tcol_1'}, dimensions={2} | all-to-all | bytes 1048576 | tf_op jit(solution)/shard_map/all_to_all | solution.py:68
  215.5 1.3 fusion.185
  218.2 1.1 copy.70
  219.3 16.7 %all_to_all.33 = bf16[1,2,1024,128]{3,1,0,2:T(2,128)(2,1)S(1)} all-to-all(bf16[1,2,1024,128]{3,1,0,2:T(2,128)(2,1)} %copy.70), channel_id=1, replica_groups=mesh['freq_0'=4,'freq_1'=2,'tcol_0'=8,'tcol_1'=4] {'tcol_0','tcol_1'}, dimensions={2} | all-to-all | bytes 1048576 | tf_op jit(solution)/shard_map/all_to_all | solution.py:72
  239.9 7.7 %psum.92 = f32[5,128]{1,0:T(8,128)S(1)} all-reduce(f32[5,128]{1,0:T(8,128)S(1)} %stack.215), channel_id=1, replica_groups=mesh['freq_0'=4,'freq_1'=2,'tcol_0'=8,'tcol_1'=4] {'freq_0'}, use_global_device_ids=true, to_apply=%region_22.0 | all-reduce | flops 640 | bytes 5120 | tf_op jit(solution)/shard_map/psum | solution.py:15
  247.7 12.9 %psum.93 = f32[5,128]{1,0:T(8,128)S(1)} all-reduce(f32[5,128]{1,0:T(8,128)S(1)} %psum.92), channel_id=1, replica_groups=mesh['freq_0'=4,'freq_1'=2,'tcol_0'=8,'tcol_1'=4] {'freq_1'}, use_global_device_ids=true, to_apply=%region_23.0 | all-reduce | flops 640 | bytes 5120 | tf_op jit(solution)/shard_map/psum | solution.py:15
  260.5 11.6 %psum.94 = f32[5,128]{1,0:T(8,128)S(1)} all-reduce(f32[5,128]{1,0:T(8,128)S(1)} %psum.93), channel_id=1, replica_groups=mesh['freq_0'=4,'freq_1'=2,'tcol_0'=8,'tcol_1'=4] {'tcol_0'}, use_global_device_ids=true, to_apply=%region_24.0 | all-reduce | flops 640 | bytes 5120 | tf_op jit(solution)/shard_map/psum | solution.py:15
  272.2 6.9 %psum.95 = f32[5,128]{1,0:T(8,128)S(1)} all-reduce(f32[5,128]{1,0:T(8,128)S(1)} %psum.94), channel_id=1, replica_groups=mesh['freq_0'=4,'freq_1'=2,'tcol_0'=8,'tcol_1'=4] {'tcol_1'}, use_global_device_ids=true, to_apply=%region_25.0 | all-reduce | flops 640 | bytes 5120 | tf_op jit(solution)/shard_map/psum | solution.py:15
  279.1 1.9 add_subtract_fusion
  281.0 2.0 copy.74
  (130 shorter events, 34.3 us)
Async XLA Ops:
  0.6 0.7 copy-start
  0.6 5.5 %copy-start.2 = (bf16[1,2,512,1024]{3,2,1,0:T(8,128)(2,1)S(1)}, bf16[1,2,512,1024]{3,2,1,0:T(8,128)(2,1)}, u32[]{:S(2)}) copy-start(bf16[1,2,512,1024]{3,2,1,0:T(8,128)(2,1)} %param.6) | copy-start | bytes 6291460
  0.7 5.5 %copy-start.23 = (bf16[1,2,512,128]{3,2,1,0:T(8,128)(2,1)S(1)}, bf16[1,2,512,128]{3,2,1,0:T(8,128)(2,1)}, u32[]{:S(2)}) copy-start(bf16[1,2,512,128]{3,2,1,0:T(8,128)(2,1)} %param.5) | copy-start | bytes 786436
  8.3 30.2 %copy-start.1 = (bf16[1,2,512,1024]{3,2,1,0:T(8,128)(2,1)S(1)}, bf16[1,2,512,1024]{3,2,1,0:T(8,128)(2,1)}, u32[]{:S(2)}) copy-start(bf16[1,2,512,1024]{3,2,1,0:T(8,128)(2,1)} %param.7) | copy-start | bytes 6291460
  9.7 28.1 %all-to-all-start = ((bf16[1,2,1024,128]{3,1,0,2:T(2,128)(2,1)}), bf16[1,2,1024,128]{3,1,0,2:T(2,128)(2,1)S(1)}, u32[]{:S(2)}, u32[]{:S(2)}) async-start(bf16[1,2,1024,128]{3,1,0,2:T(2,128)(2,1)} %copy.46), calls=%async_computation | async-start | bytes 1048576 | tf_op jit(solution)/shard_map/all_to_all | solution.py:68
  43.1 20.5 %all-to-all-start.1 = ((bf16[1,2,1024,128]{3,1,0,2:T(2,128)(2,1)}), bf16[1,2,1024,128]{3,1,0,2:T(2,128)(2,1)S(1)}, u32[]{:S(2)}, u32[]{:S(2)}) async-start(bf16[1,2,1024,128]{3,1,0,2:T(2,128)(2,1)} %copy.49), calls=%async_computation.1 | async-start | bytes 1048576 | tf_op jit(solution)/shard_map/all_to_all | solution.py:72
  49.5 53.3 %copy-start.11 = (bf16[1,2,512,128]{2,3,1,0:T(8,128)(2,1)}, bf16[1,2,512,128]{2,3,1,0:T(8,128)(2,1)S(1)}, u32[]{:S(2)}) copy-start(bf16[1,2,512,128]{2,3,1,0:T(8,128)(2,1)S(1)} %copy.52) | copy-start | bytes 786436
  63.6 1.6 copy-start.3
  102.7 2.1 copy-start.4
  127.5 0.8 copy-start.8
  131.9 17.5 %copy-start.5 = (bf16[1,2,512,1024]{3,2,1,0:T(8,128)(2,1)S(1)}, bf16[1,2,512,1024]{3,2,1,0:T(8,128)(2,1)}, u32[]{:S(2)}) copy-start(bf16[1,2,512,1024]{3,2,1,0:T(8,128)(2,1)} %param.6) | copy-start | bytes 6291460
  150.3 1.0 copy-start.9
  150.8 1.6 copy-start.20
  150.8 1.1 copy-start.12
  151.4 1.1 copy-start.21
  189.7 2.5 copy-start.6
  214.4 1.0 copy-start.10
  218.1 18.5 %copy-start.7 = (bf16[1,2,512,1024]{3,2,1,0:T(8,128)(2,1)S(1)}, bf16[1,2,512,1024]{3,2,1,0:T(8,128)(2,1)}, u32[]{:S(2)}) copy-start(bf16[1,2,512,1024]{3,2,1,0:T(8,128)(2,1)} %param.6) | copy-start | bytes 6291460
  237.7 1.1 copy-start.13
  237.7 1.2 copy-start.14
  237.7 1.3 copy-start.16
  237.7 1.5 copy-start.18
  238.7 1.2 copy-start.22
  238.7 40.3 %copy-start.15 = (f32[1,2,512,128]{2,3,1,0:T(8,128)S(1)}, f32[1,2,512,128]{2,3,1,0:T(8,128)}, u32[]{:S(2)}) copy-start(f32[1,2,512,128]{2,3,1,0:T(8,128)} %get-tuple-element.28) | copy-start | bytes 1572868
  238.8 40.3 %copy-start.17 = (f32[1,2,512,128]{2,3,1,0:T(8,128)S(1)}, f32[1,2,512,128]{2,3,1,0:T(8,128)}, u32[]{:S(2)}) copy-start(f32[1,2,512,128]{2,3,1,0:T(8,128)} %get-tuple-element.24) | copy-start | bytes 1572868
  238.8 40.3 %copy-start.19 = (f32[1,2,512,128]{2,3,1,0:T(8,128)S(1)}, f32[1,2,512,128]{2,3,1,0:T(8,128)}, u32[]{:S(2)}) copy-start(f32[1,2,512,128]{2,3,1,0:T(8,128)} %get-tuple-element.25) | copy-start | bytes 1572868
where the time goes:
time: 289 us; the launch traced here: 284 us
  blocking collectives  180 us (62%)
  waiting for transfers between devices  29.8 us (10%)
  matrix products  27.4 us (9%)
  local copies, waits for them, and re-layouts  18.1 us (6%)
  starting transfers between devices  17.1 us (6%)
  other arithmetic  9.71 us (3%)
    psum x12, blocking collectives, over_axes(): shard = lax.psum(shard, axis)  111 us
    all_to_all x2, blocking collectives, body(): lax.all_to_all(coeffs, TCOL, split_axis=2, concat_axis=2, tiled=True)  35.2 us
    all_to_all x2, blocking collectives, body(): lax.all_to_all(forward_coeffs, TCOL, split_axis=2, concat_axis=2, tiled=T...  33.4 us
    all_to_all x1, waiting for transfers between devices, body(): lax.all_to_all(coeffs, TCOL, split_axis=2, concat_axis=2, tiled=True)  15.6 us
    all_to_all x1, waiting for transfers between devices, body(): lax.all_to_all(forward_coeffs, TCOL, split_axis=2, concat_axis=2, tiled=T...  14.1 us
    all_to_all x1, starting transfers between devices, body(): lax.all_to_all(coeffs, TCOL, split_axis=2, concat_axis=2, tiled=True)  11.9 us
    unnamed x51, local copies, waits for them, and re-layouts  6.4 us
    dot_general x6, matrix products, conj_left(): jnp.einsum('ftq,fts->fqs', factor[:, 0], field[:, 1], preferred_element_t...  5.85 us
  transfers between devices with their start and end apart: 2, of which 2 were waited for; matrix products, arithmetic and copies ran while one was open for 0% of the time, Pallas kernels for 0%

commit v1 on v0

v1 whole, which is shorter than its diff:
```python
import jax
import jax.numpy as jnp
from jax import lax
from jax.experimental import pallas as pl
from jax.experimental.pallas import tpu as pltpu
from jax.sharding import PartitionSpec as P

ITERS = 3
NX = 4
NZ = 8
NF = 8
RANK = 32
TILE = 512
HALF = 64
LANES = 128
BLOCK = NX * RANK
WIDE = NZ * BLOCK
ORDER = (4, 3, 5, 2, 6, 1, 7, 0)
PLACE = {dz: p for p, dz in enumerate(ORDER)}
GROUPS = 4
SPAN = NZ // GROUPS
DXS = (2, 1, 3, 0)
CHUNK = 64
MESH = pl.DeviceIdType.MESH
F32 = jnp.float32
BF16 = jnp.bfloat16


def kernel(
    data_hbm, left_hbm, right_hbm, ranks_ref, freq_ref,
    wave_out, resid_out,
    natural, turned, rawdata, spread, total, sendbuf, recvbuf,
    grad, ngrad, nump, direction, moved, image, wave, resid,
    zsrc, zslot, xsrc, xslot, fsrc, fslot,
    load_sem, bulk_send, bulk_recv, z_send, z_recv, x_send, x_recv, f_send, f_recv,
):
    f = lax.axis_index("freq")
    t = lax.axis_index("tcol")
    z = t // NX
    x = lax.rem(t, NX)

    def peer(dz, dx):
        return lax.rem(z + dz, NZ) * NX + lax.rem(x + dx, NX)

    barrier = pltpu.get_barrier_semaphore()
    for n in range(1, NZ * NX):
        pl.semaphore_signal(
            barrier, inc=1, device_id=(f, peer(n // NX, n % NX)), device_id_type=MESH
        )
    for df in range(1, NF):
        pl.semaphore_signal(
            barrier, inc=1, device_id=(lax.rem(f + df, NF), t), device_id_type=MESH
        )

    def load(factor, source, place):
        column = pl.multiple_of(lax.rem(z + ORDER[place], NZ) * BLOCK, BLOCK)
        return [
            pltpu.make_async_copy(
                source.at[0, c, :, pl.ds(column, BLOCK)],
                natural.at[factor, pl.ds(c * TILE, TILE), pl.ds(place * BLOCK, BLOCK)],
                load_sem.at[factor, place, c],
            )
            for c in range(2)
        ]

    data_copy = pltpu.make_async_copy(data_hbm.at[0], rawdata, load_sem.at[2, 0, 0])
    data_copy.start()
    for factor, source in ((0, left_hbm), (1, right_hbm)):
        for place in range(NZ):
            for copy in load(factor, source, place):
                copy.start()

    lane = lax.broadcasted_iota(jnp.int32, (1, LANES), 1)
    lower = lane < HALF
    sign = jnp.where(lower, 1.0, -1.0).astype(F32)
    damping = 0.1 + 0.9 * freq_ref[0].astype(F32) / 229.0

    def swap(value):
        return pltpu.roll(value, HALF, 1)

    def chunks(body, carry=None):
        def step(n, c):
            rows = pl.ds(pl.multiple_of(n * CHUNK, CHUNK), CHUNK)
            low = pl.ds(pl.multiple_of(n * CHUNK + TILE, CHUNK), CHUNK)
            return body(rows, low, c)

        return lax.fori_loop(0, TILE // CHUNK, step, carry)

    def put(rows, low, value):
        spread[rows, :] = value.astype(BF16)
        spread[low, :] = (swap(value) * sign).astype(BF16)

    def bulk(h, parity, place, dx):
        dz = ORDER[place]
        there = lax.rem(x + dx, NX)
        back = PLACE[(NZ - dz) % NZ]
        start = pl.multiple_of(place * BLOCK + there * RANK, RANK)
        land = pl.multiple_of(back * BLOCK + x * RANK, RANK)
        n = place * NX + dx
        return pltpu.make_async_remote_copy(
            src_ref=sendbuf.at[h, pl.ds(start, RANK), :],
            dst_ref=recvbuf.at[h, parity, pl.ds(land, RANK), :],
            send_sem=bulk_send.at[h, n],
            recv_sem=bulk_recv.at[h, parity, back * NX + dx],
            device_id=(f, peer(dz, dx)),
            device_id_type=MESH,
        )

    def arrival(h, parity, place, dx):
        there = lax.rem(x + NX - dx, NX)
        land = pl.multiple_of(place * BLOCK + there * RANK, RANK)
        return pltpu.make_async_remote_copy(
            src_ref=sendbuf.at[h, pl.ds(0, RANK), :],
            dst_ref=recvbuf.at[h, parity, pl.ds(land, RANK), :],
            send_sem=bulk_send.at[h, 0],
            recv_sem=bulk_recv.at[h, parity, place * NX + dx],
            device_id=(f, t),
            device_id_type=MESH,
        )

    def remote_pairs(places):
        return [(p, dx) for dx in DXS for p in places if not (ORDER[p] == 0 and dx == 0)]

    def drain(h, parity):
        for place, dx in remote_pairs(range(NZ)):
            bulk(h, parity, place, dx).wait_send()

    def contract(factor, h, parity, group):
        rows = pl.ds(group * SPAN * BLOCK, SPAN * BLOCK)
        coeff = jnp.dot(turned[factor, rows, :], spread[...], preferred_element_type=F32)
        sendbuf[h, rows, :] = coeff.astype(BF16)
        places = range(group * SPAN, (group + 1) * SPAN)
        if PLACE[0] in places:
            own = pl.ds(pl.multiple_of(PLACE[0] * BLOCK + x * RANK, RANK), RANK)
            recvbuf[h, parity, own, :] = sendbuf[h, own, :]
        for place, dx in remote_pairs(places):
            bulk(h, parity, place, dx).start()

    def expand(factor, h, parity):
        for group in range(GROUPS):
            for place, dx in remote_pairs(range(group * SPAN, (group + 1) * SPAN)):
                arrival(h, parity, place, dx).wait_recv()
            rows = pl.ds(group * SPAN * BLOCK, SPAN * BLOCK)
            part = jnp.dot(
                natural[factor, :, rows], recvbuf[h, parity, rows, :], preferred_element_type=F32
            )
            if group == 0:
                total[...] = part
            else:
                total[...] += part

    def expanded(rows, low):
        return total[rows, :] - swap(total[low, :]) * sign

    def zcopy(it, h, dz):
        return pltpu.make_async_remote_copy(
            src_ref=zsrc.at[it, h], dst_ref=zslot.at[it, h, dz - 1],
            send_sem=z_send.at[it, h, dz - 1], recv_sem=z_recv.at[it, h, dz - 1],
            device_id=(f, peer(dz, 0)), device_id_type=MESH,
        )

    def xcopy(it, h, dx):
        return pltpu.make_async_remote_copy(
            src_ref=xsrc.at[it, h], dst_ref=xslot.at[it, h, dx - 1],
            send_sem=x_send.at[it, h, dx - 1], recv_sem=x_recv.at[it, h, dx - 1],
            device_id=(f, peer(0, dx)), device_id_type=MESH,
        )

    def fcopy(it, h, df):
        return pltpu.make_async_remote_copy(
            src_ref=fsrc.at[it, h], dst_ref=fslot.at[it, h, df - 1],
            send_sem=f_send.at[it, h, df - 1], recv_sem=f_recv.at[it, h, df - 1],
            device_id=(lax.rem(f + df, NF), t), device_id_type=MESH,
        )

    def gathered(copy, slot, source, it, h, count):
        for d in range(1, count):
            copy(it, h, d).wait_recv()
        sums = source[it, h]
        for d in range(1, count):
            sums = sums + slot[it, h, d - 1]
        for d in range(1, count):
            copy(it, h, d).wait_send()
        return sums

    def z_to_x(it, h):
        xsrc[it, h] = gathered(zcopy, zslot, zsrc, it, h, NZ)
        for dx in range(1, NX):
            xcopy(it, h, dx).start()

    def x_to_f(it, h):
        fsrc[it, h] = gathered(xcopy, xslot, xsrc, it, h, NX)
        for df in range(1, NF):
            fcopy(it, h, df).start()

    def scales(it, h):
        sums = gathered(fcopy, fslot, fsrc, it, h, NF)
        a11, a12, a22, b1, b2 = [sums[n] + swap(sums[n]) for n in range(5)]
        if it == 0:
            return b1 / (1.1 * a11), None
        first = 1.1 * a11
        second = 1.1 * a22
        determinant = first * second - a12 * a12
        return (b1 * second - a12 * b2) / determinant, (first * b2 - a12 * b1) / determinant

    def inner(it, h):
        def fold(value):
            return jnp.sum(value.reshape(CHUNK // 8, 8, LANES), axis=0)

        def step(rows, low, sums):
            w = expanded(rows, low)
            moved[h, rows, :] = w
            if it < ITERS - 1:
                put(rows, low, w)
            g = grad[h, rows, :]
            r = resid[h, rows, :]
            dg = damping * g
            if it == 0:
                new = (w * w + dg * g, w * r)
            else:
                q = image[h, rows, :]
                p = direction[h, rows, :]
                v = wave[h, rows, :]
                dp = damping * p
                new = (w * w + dg * g, w * q + dg * p, q * q + dp * p, w * r - dg * v, q * r - dp * v)
            return tuple(s + fold(n) for s, n in zip(sums, new, strict=True))

        count = 2 if it == 0 else 5
        sums = chunks(step, tuple(jnp.zeros((8, LANES), F32) for _ in range(count)))
        sums = [jnp.sum(s, axis=0, keepdims=True) for s in sums]
        if it == 0:
            zero = jnp.zeros((1, LANES), F32)
            sums = [sums[0], zero, zero, sums[1], zero]
        for n in range(5):
            zsrc[it, h, n] = sums[n]
        for dz in (4, 3, 5, 2, 6, 1, 7):
            zcopy(it, h, dz).start()

    data_copy.wait()

    def begin(rows, low, carry):
        real = rawdata[0, rows, :].astype(F32)
        imag = rawdata[1, rows, :].astype(F32)
        resid[0, rows, :] = jnp.where(lower, real, swap(imag))
        resid[1, rows, :] = jnp.where(lower, swap(real), imag)
        return carry

    chunks(begin)

    def turn(factor, place):
        for copy in load(factor, left_hbm if factor == 0 else right_hbm, place):
            copy.wait()
        cols = pl.ds(place * BLOCK, BLOCK)
        if factor == 0:
            column = lax.rem(z + ORDER[place], NZ)
            limit = jnp.zeros((1, LANES), jnp.int32)
            for n in range(NX):
                limit = jnp.where(lane // RANK == n, ranks_ref[0, t, column * NX + n], limit)
            keep = lax.rem(lane, RANK) < limit
            keep = jnp.where(keep, 1.0, 0.0).astype(BF16)
        for n in range(2 * TILE // BLOCK):
            rows = pl.ds(n * BLOCK, BLOCK)
            tile = natural[factor, rows, cols]
            if factor == 0:
                tile = tile * keep
                natural[factor, rows, cols] = tile
            turned[factor, cols, rows] = tile.T

    def start_rows(rows, low, carry):
        put(rows, low, resid[0, rows, :])
        return carry

    chunks(start_rows)
    for group in range(GROUPS):
        for place in range(group * SPAN, (group + 1) * SPAN):
            turn(0, place)
        if group == 0:
            pl.semaphore_wait(barrier, NZ * NX - 1 + NF - 1)
        contract(0, 0, 0, group)

    def second_rows(rows, low, carry):
        put(rows, low, resid[1, rows, :])
        return carry

    chunks(second_rows)
    for group in range(GROUPS):
        contract(0, 1, 0, group)
    for place in range(NZ):
        turn(1, place)

    for it in range(ITERS):
        def adjoint(h, carry, it=it):
            expand(1, h, 0)
            drain(h, 0)
            if it == 0:
                def step(rows, low, c):
                    g = expanded(rows, low)
                    grad[h, rows, :] = g
                    put(rows, low, g)
                    return c

                chunks(step)
            else:
                @pl.when(h == 0)
                def _():
                    z_to_x(it - 1, 1)

                alpha, beta = scales(it - 1, h)

                def step(rows, low, c):
                    g = grad[h, rows, :]
                    n = alpha * (expanded(rows, low) + damping * g)
                    p = alpha * g
                    q = alpha * moved[h, rows, :]
                    if it == 1:
                        v = p
                    else:
                        n = n + beta * nump[h, rows, :]
                        p = p + beta * direction[h, rows, :]
                        q = q + beta * image[h, rows, :]
                        v = wave[h, rows, :] + p
                    g = g - n
                    put(rows, low, g)
                    grad[h, rows, :] = g
                    nump[h, rows, :] = n
                    direction[h, rows, :] = p
                    image[h, rows, :] = q
                    wave[h, rows, :] = v
                    resid[h, rows, :] = resid[h, rows, :] - q
                    return c

                chunks(step)
            for group in range(GROUPS):
                contract(1, h, 1, group)
            if it > 0:
                @pl.when(h == 0)
                def _():
                    x_to_f(it - 1, 1)
            return carry

        lax.fori_loop(0, 2, adjoint, 0)

        if it < ITERS - 1:
            def forward(h, carry, it=it):
                expand(0, h, 1)
                drain(h, 1)
                inner(it, h)
                for group in range(GROUPS):
                    contract(0, h, 0, group)
                return carry

            lax.fori_loop(0, 2, forward, 0)
            z_to_x(it, 0)
            x_to_f(it, 0)

    last = ITERS - 1

    def final(h, carry):
        expand(0, h, 1)
        drain(h, 1)
        inner(last, h)

        @pl.when(h == 0)
        def _():
            z_to_x(last, 0)

        return carry

    lax.fori_loop(0, 2, final, 0)

    def finish(h):
        alpha, beta = scales(last, h)

        def step(rows, low, c):
            p = alpha * grad[h, rows, :] + beta * direction[h, rows, :]
            q = alpha * moved[h, rows, :] + beta * image[h, rows, :]
            v = wave[h, rows, :] + p
            r = resid[h, rows, :] - q
            if h == 0:
                wave[h, rows, :] = v
                resid[h, rows, :] = r
            else:
                for out, mine, theirs in ((wave_out, wave, v), (resid_out, resid, r)):
                    other = mine[0, rows, :]
                    out[0, 0, rows, :] = jnp.where(lower, other, swap(theirs))
                    out[0, 1, rows, :] = jnp.where(lower, swap(other), theirs)
            return c

        chunks(step)

    x_to_f(last, 0)
    z_to_x(last, 1)
    finish(0)
    x_to_f(last, 1)
    finish(1)


def body(data, left_factor, right_factor, ranks, freq_index):
    anywhere = pl.BlockSpec(memory_space=pl.ANY)
    smem = pl.BlockSpec(memory_space=pltpu.SMEM)
    vmem = pl.BlockSpec(memory_space=pltpu.VMEM)
    field = pltpu.VMEM((2, TILE, LANES), F32)
    dma = pltpu.SemaphoreType.DMA
    out = jax.ShapeDtypeStruct((1, 2, TILE, LANES), F32)
    row = (5, 1, LANES)
    return pl.pallas_call(
        kernel,
        out_shape=(out, out),
        in_specs=[anywhere, anywhere, anywhere, smem, smem],
        out_specs=(vmem, vmem),
        scratch_shapes=[
            pltpu.VMEM((2, 2 * TILE, WIDE), BF16),
            pltpu.VMEM((2, WIDE, 2 * TILE), BF16),
            pltpu.VMEM((2, TILE, LANES), BF16),
            pltpu.VMEM((2 * TILE, LANES), BF16),
            pltpu.VMEM((2 * TILE, LANES), F32),
            pltpu.VMEM((2, WIDE, LANES), BF16),
            pltpu.VMEM((2, 2, WIDE, LANES), BF16),
            field, field, field, field, field, field, field, field,
            pltpu.VMEM((ITERS, 2) + row, F32),
            pltpu.VMEM((ITERS, 2, NZ - 1) + row, F32),
            pltpu.VMEM((ITERS, 2) + row, F32),
            pltpu.VMEM((ITERS, 2, NX - 1) + row, F32),
            pltpu.VMEM((ITERS, 2) + row, F32),
            pltpu.VMEM((ITERS, 2, NF - 1) + row, F32),
            dma((3, NZ, 2)),
            dma((2, NZ * NX)),
            dma((2, 2, NZ * NX)),
            dma((ITERS, 2, NZ - 1)),
            dma((ITERS, 2, NZ - 1)),
            dma((ITERS, 2, NX - 1)),
            dma((ITERS, 2, NX - 1)),
            dma((ITERS, 2, NF - 1)),
            dma((ITERS, 2, NF - 1)),
        ],
        compiler_params=pltpu.CompilerParams(
            collective_id=0, has_side_effects=True, vmem_limit_bytes=48 * 1024 * 1024
        ),
        name="tlr_descent",
    )(data, left_factor, right_factor, ranks, freq_index)


def solution(mesh):
    spec = P("freq", None, "tcol", None)
    return jax.shard_map(
        body,
        mesh=mesh,
        in_specs=(spec, spec, spec, P("freq", None, None), P("freq")),
        out_specs=(spec, spec),
        check_vma=False,
    )
```

time: 289 us -> 123 us (0.43); the launches traced: 284 us -> 123 us
  blocking collectives: 180 us -> 0 us
  Pallas kernels: 0 us -> 115 us
  waiting for transfers between devices: 29.8 us -> 0 us
  matrix products: 27.4 us -> 0 us
  starting transfers between devices: 17.1 us -> 0 us
  local copies, waits for them, and re-layouts: 18.1 us -> 6.43 us
  other arithmetic: 9.71 us -> 0 us
    pallas_call x0 -> x1, Pallas kernels: none -> 115 us  [body(): pl.pallas_call(kernel, out_shape=(out, out), in_specs=[anywhere, anywhere...]
    psum x12 -> x0, blocking collectives: 111 us -> none  [over_axes(): shard = lax.psum(shard, axis)]
    all_to_all x4 -> x0, blocking collectives: 68.6 us -> none  [the longest x2 35.2 us: body(): lax.all_to_all(coeffs, TCOL, split_axis=2, concat_axis=2, tiled=True)]
    all_to_all x2 -> x0, waiting for transfers between devices: 29.8 us -> none  [the longest x1 15.6 us: body(): lax.all_to_all(coeffs, TCOL, split_axis=2, concat_axis=2, tiled=True)]
    dot_general x48 -> x0, matrix products: 27.4 us -> none  [the longest x6 5.85 us: conj_left(): jnp.einsum('ftq,fts->fqs', factor[:, 0], field[:, 1], preferred_element_t...]
    all_to_all x2 -> x0, starting transfers between devices: 17.1 us -> none  [the longest x1 11.9 us: body(): lax.all_to_all(coeffs, TCOL, split_axis=2, concat_axis=2, tiled=True)]
    convert_element_type x6 -> x0, local copies, waits for them, and re-layouts: 6.65 us -> none  [the longest x3 4.23 us: body(): (forward_coeffs * colmask[:, None, :, None]).astype(jnp.bfloat16)]
    convert_element_type x12 -> x0, other arithmetic: 5.79 us -> none  [the longest x2 2.57 us: body(): coeffs = conj_left(left_factor, residual.astype(jnp.bfloat16))]
  transfers between devices with their start and end apart: 2 -> 0, of which waited for: 2 -> 0; matrix products, arithmetic and copies ran while one was open for 0% -> 0% of each run, Pallas kernels for 0% -> 0%
where the time goes in v1:
time: 123 us
  Pallas kernels  115 us (93%)
  local copies, waits for them, and re-layouts  6.43 us (5%)
  between operations  1.3 us (1%)
    pallas_call x1, Pallas kernels, body(): pl.pallas_call(kernel, out_shape=(out, out), in_specs=[anywhere, anywhere...  115 us
    unnamed x10, local copies, waits for them, and re-layouts  6.43 us

profile of v1, /device:TPU:1, one launch (start us, length us, event | category | flops | bytes accessed | tf_op | source)
XLA Modules:
  0.0 123.0 jit_solution(120259609977031373)
XLA Ops:
  1.3 0.0 copy-start
  1.3 1.6 %copy-done = bf16[1,2,512,1024]{3,2,1,0:T(8,128)(2,1)S(1)} copy-done((bf16[1,2,512,1024]{3,2,1,0:T(8,128)(2,1)S(1)}, bf16[1,2,512,1024]{3,2,1,0:T(8,128)(2,1)}, u32[]{:S(2)}) %copy-start) | copy-done | bytes 2097176
  2.9 0.0 copy-start.1
  2.9 1.6 %copy-done.1 = bf16[1,2,512,1024]{3,2,1,0:T(8,128)(2,1)S(1)} copy-done((bf16[1,2,512,1024]{3,2,1,0:T(8,128)(2,1)S(1)}, bf16[1,2,512,1024]{3,2,1,0:T(8,128)(2,1)}, u32[]{:S(2)}) %copy-start.1) | copy-done | bytes 2097176
  4.5 0.0 copy-start.2
  4.5 0.9 copy-done.2
  5.4 0.0 copy-start.3
  5.4 0.7 copy-done.3
  6.1 115.3 %tlr_descent.1 = (f32[1,2,512,128]{3,2,1,0:T(8,128)S(1)}, f32[1,2,512,128]{3,2,1,0:T(8,128)S(1)}) custom-call(bf16[1,2,512,128]{3,2,1,0:T(8,128)(2,1)S(1)} %copy-done.2, bf16[1,2,512,1024]{3,2,1,0:T(8,128)(2,1)S(1)} %copy-done, bf16[1,2,512,1024]{3,2,1,0:T(8,128)(2,1)S(1)} %copy-done.1, s32[1,32,32]{2,1,0:T(8,128)S(1)} %copy-done.3, s32[1]{0:T(128)S(6)} %copy.9.freq_ref), custom_call_target="tpu_custom_call" | custom-call | tf_op jit(solution)/shard_map/tlr_descent/pallas_call | solution.py:406
  121.4 0.8 copy.10
  122.2 0.8 copy.11
Async XLA Ops:
  1.3 1.6 %copy-start = (bf16[1,2,512,1024]{3,2,1,0:T(8,128)(2,1)S(1)}, bf16[1,2,512,1024]{3,2,1,0:T(8,128)(2,1)}, u32[]{:S(2)}) copy-start(bf16[1,2,512,1024]{3,2,1,0:T(8,128)(2,1)} %left_hbm.1) | copy-start | bytes 6291460
  2.9 1.6 %copy-start.1 = (bf16[1,2,512,1024]{3,2,1,0:T(8,128)(2,1)S(1)}, bf16[1,2,512,1024]{3,2,1,0:T(8,128)(2,1)}, u32[]{:S(2)}) copy-start(bf16[1,2,512,1024]{3,2,1,0:T(8,128)(2,1)} %right_hbm.1) | copy-start | bytes 6291460
  4.5 0.9 copy-start.2
  5.4 0.7 copy-start.3

commit v2 on v1

--- a/solution.py
+++ b/solution.py
@@ -18,6 +18,7 @@
 ORDER = (4, 3, 5, 2, 6, 1, 7, 0)
 PLACE = {dz: p for p, dz in enumerate(ORDER)}
 GROUPS = 4
+PARTS = 2
 SPAN = NZ // GROUPS
 DXS = (2, 1, 3, 0)
 CHUNK = 64
@@ -30,9 +31,9 @@
     data_hbm, left_hbm, right_hbm, ranks_ref, freq_ref,
     wave_out, resid_out,
     natural, turned, rawdata, spread, total, sendbuf, recvbuf,
-    grad, ngrad, nump, direction, moved, image, wave, resid,
-    zsrc, zslot, xsrc, xslot, fsrc, fslot,
-    load_sem, bulk_send, bulk_recv, z_send, z_recv, x_send, x_recv, f_send, f_recv,
+    grad, ngrad, nump, knump, direction, moved, image, wave, resid,
+    zsrc, zslot, xsrc, xslot, fsrc, fslot, asrc, aslot,
+    load_sem, bulk_send, bulk_recv, z_send, z_recv, x_send, x_recv, f_send, f_recv, a_send, a_recv,
 ):
     f = lax.axis_index("freq")
     t = lax.axis_index("tcol")
@@ -98,9 +99,9 @@
         land = pl.multiple_of(back * BLOCK + x * RANK, RANK)
         n = place * NX + dx
         return pltpu.make_async_remote_copy(
-            src_ref=sendbuf.at[h, pl.ds(start, RANK), :],
+            src_ref=sendbuf.at[h, parity, pl.ds(start, RANK), :],
             dst_ref=recvbuf.at[h, parity, pl.ds(land, RANK), :],
-            send_sem=bulk_send.at[h, n],
+            send_sem=bulk_send.at[h, parity, n],
             recv_sem=bulk_recv.at[h, parity, back * NX + dx],
             device_id=(f, peer(dz, dx)),
             device_id_type=MESH,
@@ -110,9 +111,9 @@
         there = lax.rem(x + NX - dx, NX)
         land = pl.multiple_of(place * BLOCK + there * RANK, RANK)
         return pltpu.make_async_remote_copy(
-            src_ref=sendbuf.at[h, pl.ds(0, RANK), :],
+            src_ref=sendbuf.at[h, parity, pl.ds(0, RANK), :],
             dst_ref=recvbuf.at[h, parity, pl.ds(land, RANK), :],
-            send_sem=bulk_send.at[h, 0],
+            send_sem=bulk_send.at[h, parity, 0],
             recv_sem=bulk_recv.at[h, parity, place * NX + dx],
             device_id=(f, t),
             device_id_type=MESH,
@@ -125,14 +126,15 @@
         for place, dx in remote_pairs(range(NZ)):
             bulk(h, parity, place, dx).wait_send()
 
-    def contract(factor, h, parity, group):
-        rows = pl.ds(group * SPAN * BLOCK, SPAN * BLOCK)
+    def contract(factor, h, parity, group, groups):
+        span = NZ // groups
+        rows = pl.ds(group * span * BLOCK, span * BLOCK)
         coeff = jnp.dot(turned[factor, rows, :], spread[...], preferred_element_type=F32)
-        sendbuf[h, rows, :] = coeff.astype(BF16)
-        places = range(group * SPAN, (group + 1) * SPAN)
+        sendbuf[h, parity, rows, :] = coeff.astype(BF16)
+        places = range(group * span, (group + 1) * span)
         if PLACE[0] in places:
             own = pl.ds(pl.multiple_of(PLACE[0] * BLOCK + x * RANK, RANK), RANK)
-            recvbuf[h, parity, own, :] = sendbuf[h, own, :]
+            recvbuf[h, parity, own, :] = sendbuf[h, parity, own, :]
         for place, dx in remote_pairs(places):
             bulk(h, parity, place, dx).start()
 
@@ -183,19 +185,41 @@
             copy(it, h, d).wait_send()
         return sums
 
+    def acopy(h, dz, dx):
+        n = dz * NX + dx - 1
+        return pltpu.make_async_remote_copy(
+            src_ref=asrc.at[h], dst_ref=aslot.at[h, n],
+            send_sem=a_send.at[h, n], recv_sem=a_recv.at[h, n],
+            device_id=(f, peer(dz, dx)), device_id_type=MESH,
+        )
+
+    def f_to_z(it, h):
+        zsrc[it, h] = gathered(fcopy, fslot, fsrc, it, h, NF)
+        for dz in (4, 3, 5, 2, 6, 1, 7):
+            zcopy(it, h, dz).start()
+
     def z_to_x(it, h):
         xsrc[it, h] = gathered(zcopy, zslot, zsrc, it, h, NZ)
         for dx in range(1, NX):
             xcopy(it, h, dx).start()
 
-    def x_to_f(it, h):
-        fsrc[it, h] = gathered(xcopy, xslot, xsrc, it, h, NX)
-        for df in range(1, NF):
-            fcopy(it, h, df).start()
+    def f_to_all(it, h):
+        asrc[h] = gathered(fcopy, fslot, fsrc, it, h, NF)
+        for p, dx in remote_pairs(range(NZ)):
+            acopy(h, ORDER[p], dx).start()
 
     def scales(it, h):
-        sums = gathered(fcopy, fslot, fsrc, it, h, NF)
-        a11, a12, a22, b1, b2 = [sums[n] + swap(sums[n]) for n in range(5)]
+        if it < ITERS - 1:
+            sums = gathered(xcopy, xslot, xsrc, it, h, NX)
+        else:
+            for p, dx in remote_pairs(range(NZ)):
+                acopy(h, ORDER[p], dx).wait_recv()
+            sums = asrc[h] + jnp.sum(aslot[h], axis=0)
+            for p, dx in remote_pairs(range(NZ)):
+                acopy(h, ORDER[p], dx).wait_send()
+        packed = [sums[n] for n in range(3)]
+        a11, a22, b2 = [jnp.where(lower, s, swap(s)) for s in packed]
+        b1, a12 = [jnp.where(lower, swap(s), s) for s in packed[:2]]
         if it == 0:
             return b1 / (1.1 * a11), None
         first = 1.1 * a11
@@ -203,38 +227,23 @@
         determinant = first * second - a12 * a12
         return (b1 * second - a12 * b2) / determinant, (first * b2 - a12 * b1) / determinant
 
-    def inner(it, h):
-        def fold(value):
-            return jnp.sum(value.reshape(CHUNK // 8, 8, LANES), axis=0)
-
-        def step(rows, low, sums):
-            w = expanded(rows, low)
-            moved[h, rows, :] = w
-            if it < ITERS - 1:
-                put(rows, low, w)
-            g = grad[h, rows, :]
-            r = resid[h, rows, :]
-            dg = damping * g
-            if it == 0:
-                new = (w * w + dg * g, w * r)
-            else:
-                q = image[h, rows, :]
-                p = direction[h, rows, :]
-                v = wave[h, rows, :]
-                dp = damping * p
-                new = (w * w + dg * g, w * q + dg * p, q * q + dp * p, w * r - dg * v, q * r - dp * v)
-            return tuple(s + fold(n) for s, n in zip(sums, new, strict=True))
-
-        count = 2 if it == 0 else 5
-        sums = chunks(step, tuple(jnp.zeros((8, LANES), F32) for _ in range(count)))
-        sums = [jnp.sum(s, axis=0, keepdims=True) for s in sums]
-        if it == 0:
-            zero = jnp.zeros((1, LANES), F32)
-            sums = [sums[0], zero, zero, sums[1], zero]
-        for n in range(5):
-            zsrc[it, h, n] = sums[n]
-        for dz in (4, 3, 5, 2, 6, 1, 7):
-            zcopy(it, h, dz).start()
+    def fold(value):
+        return jnp.sum(value.reshape(CHUNK // 8, 8, LANES), axis=0)
+
+    def announce(it, h, a11, b1, a22, a12, b2):
+        sums = [jnp.sum(s, axis=0, keepdims=True) for s in (a11, b1, a22, a12, b2)]
+        sums = [s + swap(s) for s in sums]
+        fsrc[it, h, 0] = jnp.where(lower, sums[0], sums[1])
+        fsrc[it, h, 1] = jnp.where(lower, sums[2], sums[3])
+        fsrc[it, h, 2] = sums[4]
+        for df in range(1, NF):
+            fcopy(it, h, df).start()
+
+    def blank(count):
+        return tuple(jnp.zeros((8, LANES), F32) for _ in range(count))
+
+    def add(sums, new):
+        return tuple(s + fold(n) for s, n in zip(sums, new, strict=True))
 
     data_copy.wait()
 
@@ -276,97 +285,149 @@
             turn(0, place)
         if group == 0:
             pl.semaphore_wait(barrier, NZ * NX - 1 + NF - 1)
-        contract(0, 0, 0, group)
+        contract(0, 0, 0, group, GROUPS)
 
     def second_rows(rows, low, carry):
         put(rows, low, resid[1, rows, :])
         return carry
 
     chunks(second_rows)
-    for group in range(GROUPS):
-        contract(0, 1, 0, group)
+    for group in range(PARTS):
+        contract(0, 1, 0, group, PARTS)
     for place in range(NZ):
         turn(1, place)
 
-    for it in range(ITERS):
+    def first_adjoint(h, carry):
+        expand(1, h, 0)
+
+        def step(rows, low, c):
+            g = expanded(rows, low)
+            grad[h, rows, :] = g
+            put(rows, low, g)
+            return c
+
+        chunks(step)
+        for group in range(PARTS):
+            contract(1, h, 1, group, PARTS)
+        drain(h, 0)
+        return carry
+
+    def first_forward(h, carry):
+        expand(0, h, 1)
+
+        def step(rows, low, sums):
+            w = expanded(rows, low)
+            moved[h, rows, :] = w
+            put(rows, low, w)
+            g = grad[h, rows, :]
+            return add(sums, (w * w + damping * g * g, w * resid[h, rows, :]))
+
+        a11, b1 = chunks(step, blank(2))
+        announce(0, h, a11, b1, *blank(3))
+
+        @pl.when(h == 1)
+        def _():
+            f_to_z(0, 0)
+
+        for group in range(PARTS):
+            contract(0, h, 0, group, PARTS)
+        drain(h, 1)
+        return carry
+
+    lax.fori_loop(0, 2, first_adjoint, 0)
+    lax.fori_loop(0, 2, first_forward, 0)
+
+    for it in range(ITERS - 1):
         def adjoint(h, carry, it=it):
             expand(1, h, 0)
+
+            def step(rows, low, c):
+                n = expanded(rows, low) + damping * grad[h, rows, :]
+                ngrad[h, rows, :] = n
+                put(rows, low, n)
+                return c
+
+            chunks(step)
+
+            @pl.when(h == 0)
+            def _():
+                f_to_z(it, 1)
+
+            @pl.when(h == 1)
+            def _():
+                z_to_x(it, 0)
+
+            for group in range(PARTS):
+                contract(1, h, 1, group, PARTS)
             drain(h, 0)
-            if it == 0:
-                def step(rows, low, c):
-                    g = expanded(rows, low)
-                    grad[h, rows, :] = g
-                    put(rows, low, g)
-                    return c
-
-                chunks(step)
-            else:
-                @pl.when(h == 0)
-                def _():
-                    z_to_x(it - 1, 1)
-
-                alpha, beta = scales(it - 1, h)
-
-                def step(rows, low, c):
-                    g = grad[h, rows, :]
-                    n = alpha * (expanded(rows, low) + damping * g)
-                    p = alpha * g
-                    q = alpha * moved[h, rows, :]
-                    if it == 1:
-                        v = p
-                    else:
-                        n = n + beta * nump[h, rows, :]
-                        p = p + beta * direction[h, rows, :]
-                        q = q + beta * image[h, rows, :]
-                        v = wave[h, rows, :] + p
-                    g = g - n
-                    put(rows, low, g)
-                    grad[h, rows, :] = g
-                    nump[h, rows, :] = n
-                    direction[h, rows, :] = p
-                    image[h, rows, :] = q
-                    wave[h, rows, :] = v
-                    resid[h, rows, :] = resid[h, rows, :] - q
-                    return c
-
-                chunks(step)
-            for group in range(GROUPS):
-                contract(1, h, 1, group)
-            if it > 0:
-                @pl.when(h == 0)
-                def _():
-                    x_to_f(it - 1, 1)
+
+            @pl.when(h == 1)
+            def _():
+                z_to_x(it, 1)
+
             return carry
 
+        def forward(h, carry, it=it):
+            alpha, beta = scales(it, h)
+
+            def update(rows, low, sums):
+                g = grad[h, rows, :]
+                n = alpha * ngrad[h, rows, :]
+                p = alpha * g
+                q = alpha * moved[h, rows, :]
+                if it == 0:
+                    v = p
+                else:
+                    n = n + beta * nump[h, rows, :]
+                    p = p + beta * direction[h, rows, :]
+                    q = q + beta * image[h, rows, :]
+                    v = wave[h, rows, :] + p
+                g = g - n
+                r = resid[h, rows, :] - q
+                grad[h, rows, :] = g
+                nump[h, rows, :] = n
+                direction[h, rows, :] = p
+                image[h, rows, :] = q
+                wave[h, rows, :] = v
+                resid[h, rows, :] = r
+                dg = damping * g
+                dp = damping * p
+                return add(sums, (dg * g, dg * p, q * q + dp * p, -dg * v, q * r - dp * v))
+
+            sums = chunks(update, blank(5))
+            expand(0, h, 1)
+
+            def step(rows, low, sums):
+                k = alpha * expanded(rows, low)
+                if it > 0:
+                    k = k + beta * knump[h, rows, :]
+                w = moved[h, rows, :] - k
+                moved[h, rows, :] = w
+                if it < ITERS - 2:
+                    knump[h, rows, :] = k
+                    put(rows, low, w)
+                return add(sums, (w * w, w * image[h, rows, :], w * resid[h, rows, :]))
+
+            a11, a12, b1 = chunks(step, (sums[0], sums[1], sums[3]))
+            announce(it + 1, h, a11, b1, sums[2], a12, sums[4])
+
+            @pl.when(h == 1)
+            def _():
+                if it < ITERS - 2:
+                    f_to_z(it + 1, 0)
+                else:
+                    f_to_all(it + 1, 0)
+
+            if it < ITERS - 2:
+                for group in range(PARTS):
+                    contract(0, h, 0, group, PARTS)
+            drain(h, 1)
+            return carry
+
         lax.fori_loop(0, 2, adjoint, 0)
-
-        if it < ITERS - 1:
-            def forward(h, carry, it=it):
-                expand(0, h, 1)
-                drain(h, 1)
-                inner(it, h)
-                for group in range(GROUPS):
-                    contract(0, h, 0, group)
-                return carry
-
-            lax.fori_loop(0, 2, forward, 0)
-            z_to_x(it, 0)
-            x_to_f(it, 0)
+        lax.fori_loop(0, 2, forward, 0)
 
     last = ITERS - 1
-
-    def final(h, carry):
-        expand(0, h, 1)
-        drain(h, 1)
-        inner(last, h)
-
-        @pl.when(h == 0)
-        def _():
-            z_to_x(last, 0)
-
-        return carry
-
-    lax.fori_loop(0, 2, final, 0)
 
     def finish(h):
         alpha, beta = scales(last, h)
@@ -388,22 +449,40 @@
 
         chunks(step)
 
-    x_to_f(last, 0)
-    z_to_x(last, 1)
+    f_to_all(last, 1)
     finish(0)
-    x_to_f(last, 1)
     finish(1)
 
 
+def relay(wave_in, resid_in, wave_out, resid_out, held, in_sem, out_sem):
+    pieces = [(n, c) for n in range(2) for c in range(2)]
+    sources, targets = (wave_in, resid_in), (wave_out, resid_out)
+    loads = [
+        pltpu.make_async_copy(sources[n].at[0, c], held.at[n, c], in_sem.at[n, c])
+        for n, c in pieces
+    ]
+    stores = [
+        pltpu.make_async_copy(held.at[n, c], targets[n].at[0, c], out_sem.at[n, c])
+        for n, c in pieces
+    ]
+    for load in loads:
+        load.start()
+    for load, store in zip(loads, stores, strict=True):
+        load.wait()
+        store.start()
+    for store in stores:
+        store.wait()
+
+
 def body(data, left_factor, right_factor, ranks, freq_index):
-    anywhere = pl.BlockSpec(memory_space=pl.ANY)
+    anywhere = pl.BlockSpec(memory_space=pltpu.HBM)
     smem = pl.BlockSpec(memory_space=pltpu.SMEM)
     vmem = pl.BlockSpec(memory_space=pltpu.VMEM)
     field = pltpu.VMEM((2, TILE, LANES), F32)
     dma = pltpu.SemaphoreType.DMA
     out = jax.ShapeDtypeStruct((1, 2, TILE, LANES), F32)
-    row = (5, 1, LANES)
-    return pl.pallas_call(
+    row = (3, 1, LANES)
+    results = pl.pallas_call(
         kernel,
         out_shape=(out, out),
         in_specs=[anywhere, anywhere, anywhere, smem, smem],
@@ -414,17 +493,19 @@
             pltpu.VMEM((2, TILE, LANES), BF16),
             pltpu.VMEM((2 * TILE, LANES), BF16),
             pltpu.VMEM((2 * TILE, LANES), F32),
-            pltpu.VMEM((2, WIDE, LANES), BF16),
             pltpu.VMEM((2, 2, WIDE, LANES), BF16),
-            field, field, field, field, field, field, field, field,
+            pltpu.VMEM((2, 2, WIDE, LANES), BF16),
+            field, field, field, field, field, field, field, field, field,
             pltpu.VMEM((ITERS, 2) + row, F32),
             pltpu.VMEM((ITERS, 2, NZ - 1) + row, F32),
             pltpu.VMEM((ITERS, 2) + row, F32),
             pltpu.VMEM((ITERS, 2, NX - 1) + row, F32),
             pltpu.VMEM((ITERS, 2) + row, F32),
             pltpu.VMEM((ITERS, 2, NF - 1) + row, F32),
+            pltpu.VMEM((2,) + row, F32),
+            pltpu.VMEM((2, NZ * NX - 1) + row, F32),
             dma((3, NZ, 2)),
-            dma((2, NZ * NX)),
+            dma((2, 2, NZ * NX)),
             dma((2, 2, NZ * NX)),
             dma((ITERS, 2, NZ - 1)),
             dma((ITERS, 2, NZ - 1)),
@@ -432,12 +513,22 @@
             dma((ITERS, 2, NX - 1)),
             dma((ITERS, 2, NF - 1)),
             dma((ITERS, 2, NF - 1)),
+            dma((2, NZ * NX - 1)),
+            dma((2, NZ * NX - 1)),
         ],
         compiler_params=pltpu.CompilerParams(
-            collective_id=0, has_side_effects=True, vmem_limit_bytes=48 * 1024 * 1024
+            collective_id=0, has_side_effects=True, vmem_limit_bytes=67043328
         ),
         name="tlr_descent",
     )(data, left_factor, right_factor, ranks, freq_index)
+    return pl.pallas_call(
+        relay,
+        out_shape=(out, out),
+        in_specs=[anywhere, anywhere],
+        out_specs=(anywhere, anywhere),
+        scratch_shapes=[pltpu.VMEM((2, 2, TILE, LANES), F32), dma((2, 2)), dma((2, 2))],
+        name="relay",
+    )(*results)
 
 
 def solution(mesh):

time: 123 us -> 107 us (0.87)
  Pallas kernels: 115 us -> 105 us
  local copies, waits for them, and re-layouts: 6.43 us -> 0 us
    pallas_call x1, Pallas kernels: 115 us -> 103 us  [body(): pl.pallas_call(kernel, out_shape=(out, out), in_specs=[anywhere, anywhere...]
    unnamed x10 -> x0, local copies, waits for them, and re-layouts: 6.43 us -> none
    pallas_call x0 -> x1, Pallas kernels: none -> 1.98 us  [body(): pl.pallas_call(relay, out_shape=(out, out), in_specs=[anywhere, anywhere]...]
where the time goes in v2:
time: 107 us
  Pallas kernels  105 us (98%)
  between operations  1.45 us (1%)
    pallas_call x1, Pallas kernels, body(): pl.pallas_call(kernel, out_shape=(out, out), in_specs=[anywhere, anywhere...  103 us

profile of v2, /device:TPU:1, one launch (start us, length us, event | category | flops | bytes accessed | tf_op | source)
XLA Modules:
  0.0 106.5 jit_solution(4437277444018788738)
XLA Ops:
  1.3 103.1 %tlr_descent.1 = (f32[1,2,512,128]{3,2,1,0:T(8,128)}, f32[1,2,512,128]{3,2,1,0:T(8,128)}) custom-call(bf16[1,2,512,128]{3,2,1,0:T(8,128)(2,1)} %data_hbm.1, bf16[1,2,512,1024]{3,2,1,0:T(8,128)(2,1)} %left_hbm.1, bf16[1,2,512,1024]{3,2,1,0:T(8,128)(2,1)} %right_hbm.1, s32[1,32,32]{2,1,0:T(8,128)} %ranks_ref.1, s32[1]{0:T(128)S(6)} %copy.7.freq_ref), custom_call_target="tpu_custom_call" | custom-call | tf_op jit(solution)/shard_map/tlr_descent/pallas_call | solution.py:485
  104.4 2.0 %relay.1 = (f32[1,2,512,128]{3,2,1,0:T(8,128)}, f32[1,2,512,128]{3,2,1,0:T(8,128)}) custom-call(f32[1,2,512,128]{3,2,1,0:T(8,128)} %get-tuple-element.4.wave_in, f32[1,2,512,128]{3,2,1,0:T(8,128)} %get-tuple-element.5.resid_in), custom_call_target="tpu_custom_call" | custom-call | tf_op jit(solution)/shard_map/relay/pallas_call | solution.py:524
